TPU v7x, 32 devices: a whole 2x2x4 slice. The times are simulated.
32 devices in a mesh: feat: 8 (over z, y), row: 2 (over x), col: 2 (over core).
Axes of the slice: x: 2, y: 2, z: 4, core: 2. Of those that a mesh axis runs over, the one named last changes fastest.
Arguments:
- local_x: float32 [4, 32, 256], P(('row', 'col'), 'feat'), may hold values from -4 to 4
- dual_var: float32 [4, 32, 256], P(('row', 'col'), 'feat'), may hold values from -2 to 2
- consensus_old: float32 [32, 256], P('feat'), may hold values from -4 to 4
- blocks_data: bfloat16 [4, 32, 512, 256], P(('row', 'col'), 'feat'), may hold values from -0.375 to 0.375
- row_index: int32 [4, 32, 512], P(('row', 'col'), 'feat'), may hold values from 0 to 16383, as said below
- labels: int32 [4, 16384], P(('row', 'col')), may hold values 0 or 1
Outputs:
- solved_x: float32 [4, 32, 256], P(('row', 'col'), 'feat')
- dual_new: float32 [4, 32, 256], P(('row', 'col'), 'feat')
- consensus: float32 [32, 256], P('feat')
- norms: float32 [2], replicated
Inputs may be any that keep to these rules, and one draw needn't show every extreme that they name: `row_index`: the 512 rows of one block are distinct samples of its shard; a sample may appear in no block or in several.
All inputs are finite; a program needn't handle non-finite values. No bound on the sum of `labels` on one device may be relied on, other than what follows from the above.
Results may differ from a plain program's by a relative error of at most 0.0019.
Values sent between devices are 32-bit elements; how exact they have to be, the bound alone decides.
A program may use at most 64 MiB of HBM per device.

v0:
```python
import jax
import jax.numpy as jnp
from jax import lax
from jax.sharding import PartitionSpec as P

NEWTON_STEPS = 2
CG_STEPS = 3
penalty = 1.0
damping = 0.5
threshold = 0.05


def shrink(values):
    return jnp.sign(values) * jnp.maximum(jnp.abs(values) - threshold, 0.0)


def conjugate_solve(hessian, gradient):
    delta = jnp.zeros_like(gradient)
    residual = gradient
    direction = gradient
    power = jnp.sum(residual * residual, axis=1)
    for cg_step in range(CG_STEPS):
        image = jnp.einsum("bkl,bl->bk", hessian, direction, precision=lax.Precision.HIGHEST)
        alpha = power / jnp.sum(direction * image, axis=1)
        delta = delta + alpha[:, None] * direction
        residual = residual - alpha[:, None] * image
        power_next = jnp.sum(residual * residual, axis=1)
        direction = residual + (power_next / power)[:, None] * direction
        power = power_next
    return delta


def local(local_x, dual_var, consensus_old, blocks_data, row_index, labels):
    iterate = local_x[0]
    dual_local = dual_var[0]
    block_rows = blocks_data[0]
    index_rows = row_index[0]
    targets = labels[0].astype(jnp.float32)
    samples = targets.shape[0]
    target = consensus_old - dual_local
    flat_index = index_rows.reshape(-1)
    identity = jnp.eye(iterate.shape[1], dtype=jnp.float32)
    for newton_step in range(NEWTON_STEPS):
        rounded = iterate.astype(jnp.bfloat16)
        partial_value = jnp.einsum(
            "brk,bk->br", block_rows, rounded, preferred_element_type=jnp.float32
        )
        local_margins = jax.ops.segment_sum(
            partial_value.reshape(-1), flat_index, num_segments=samples
        )
        margins = lax.psum(local_margins, "feat")
        prob = jax.nn.sigmoid(margins)
        misfit = prob - targets
        weights = prob * (1.0 - prob)
        misfit_rows = misfit[index_rows].astype(jnp.bfloat16)
        gradient = jnp.einsum(
            "brk,br->bk", block_rows, misfit_rows, preferred_element_type=jnp.float32
        )
        gradient = gradient + penalty * (iterate - target)
        weighted = (block_rows * weights[index_rows][:, :, None]).astype(jnp.bfloat16)
        hessian = (
            jnp.einsum("brk,brl->bkl", block_rows, weighted, preferred_element_type=jnp.float32)
            + penalty * identity
        )
        delta = conjugate_solve(hessian, gradient)
        iterate = iterate - damping * delta
    shards = lax.axis_size(("row", "col"))
    combined = iterate + dual_local
    totals = lax.psum(combined, ("row", "col"))
    consensus = shrink(totals / jnp.float32(shards))
    dual_next = dual_local + iterate - consensus
    primal_local = jnp.sum((iterate - consensus) ** 2)
    change_local = jnp.sum((consensus - consensus_old) ** 2)
    primal_total, change_total = lax.psum(
        (primal_local, change_local / jnp.float32(shards)), ("feat", "row", "col")
    )
    norms = jnp.stack(
        [jnp.sqrt(primal_total), penalty * jnp.sqrt(jnp.float32(shards) * change_total)]
    )
    return (iterate[None], dual_next[None], consensus, norms)


def solution(mesh):
    placed = (
        P(("row", "col"), "feat", None),
        P(("row", "col"), "feat", None),
        P("feat", None),
        P(("row", "col"), "feat", None, None),
        P(("row", "col"), "feat", None),
        P(("row", "col"), None),
    )
    return jax.shard_map(
        local,
        mesh=mesh,
        in_specs=placed,
        out_specs=(
            P(("row", "col"), "feat", None),
            P(("row", "col"), "feat", None),
            P("feat", None),
            P(),
        ),
        check_vma=False,
    )
```

profile of v0, /device:TPU:0, one launch (start us, length us, event | category | flops | bytes accessed | tf_op | source)
XLA Modules:
  0.0 292.5 jit_solution(3661908139111151564)
XLA Ops:
  7.2 0.7 fusion.62
  7.9 1.6 fusion.26
  9.6 11.8 %scatter_custom_fusion = f32[16384]{0:T(1024)} fusion(s32[2048]{0:T(1024)S(1)} %bitcast.146, f32[2048]{0:T(1024)S(1)} %bitcast.149, f32[]{:T(128)} %constant.9.clone.1), kind=kCustom, calls=%fused_computation.36 | custom fusion | flops 2048 | bytes 65540 | tf_op jit(solution)/shard_map/scatter-add | solution.py:48
  21.6 72.0 %all-reduce.4.cloned.1.call-done = f32[16384]{0:T(1024)} async-done(((f32[16384]{0:T(1024)}), f32[16384]{0:T(1024)}) %all-reduce.4.cloned.1.call-update) | async-done | bytes 65552 | tf_op jit(solution)/shard_map/psum | solution.py:51
  93.5 0.9 subtract_multiply_fusion.1
  94.4 11.8 %gather_fusion.1 = f32[2048]{0:T(1024)S(1)} fusion(f32[16384]{0:T(1024)S(1)} %subtract_multiply_fusion.1, s32[2048]{0:T(1024)S(1)} %broadcast_clamp_fusion), kind=kCustom, calls=%fused_computation.1 | custom fusion | bytes 24576 | tf_op jit(solution)/shard_map/gather | solution.py:60
  106.3 13.1 %gather_fusion = bf16[2048]{0:T(1024)(128)(2,1)S(1)} fusion(bf16[16384]{0:T(1024)(128)(2,1)S(1)} %fusion.35, s32[2048]{0:T(1024)S(1)} %broadcast_clamp_fusion), kind=kCustom, calls=%fused_computation | custom fusion | bytes 16384 | tf_op jit(solution)/shard_map/gather | solution.py:55
  119.7 0.9 fusion.9
  120.6 0.7 fusion.59
  121.7 0.7 fusion.57
  122.8 0.7 fusion.55
  124.1 11.8 %scatter_custom_fusion.1 = f32[16384]{0:T(1024)} fusion(s32[2048]{0:T(1024)S(1)} %bitcast.147, f32[2048]{0:T(1024)S(1)} %bitcast.148, f32[]{:T(128)} %constant.9.clone.1), kind=kCustom, calls=%fused_computation.34 | custom fusion | flops 2048 | bytes 65540 | tf_op jit(solution)/shard_map/scatter-add | solution.py:48
  135.9 69.3 %all-reduce.6.cloned.1.call-done = f32[16384]{0:T(1024)} async-done(((f32[16384]{0:T(1024)}), f32[16384]{0:T(1024)}) %all-reduce.6.cloned.1.call-update) | async-done | bytes 65552 | tf_op jit(solution)/shard_map/psum | solution.py:51
  205.3 0.9 fusion.36
  206.2 13.1 %gather_fusion.2 = bf16[2048]{0:T(1024)(128)(2,1)S(1)} fusion(bf16[16384]{0:T(1024)(128)(2,1)S(1)} %fusion.36, s32[2048]{0:T(1024)S(1)} %broadcast_clamp_fusion), kind=kCustom, calls=%fused_computation.2 | custom fusion | bytes 16384 | tf_op jit(solution)/shard_map/gather | solution.py:55
  219.3 11.8 %gather_fusion.3 = f32[2048]{0:T(1024)S(1)} fusion(f32[16384]{0:T(1024)S(1)} %subtract_multiply_fusion, s32[2048]{0:T(1024)S(1)} %broadcast_clamp_fusion), kind=kCustom, calls=%fused_computation.3 | custom fusion | bytes 24576 | tf_op jit(solution)/shard_map/gather | solution.py:60
  231.3 0.9 fusion.15
  232.3 0.7 fusion.52
  233.4 0.7 fusion.50
  234.5 0.7 fusion.48
  235.3 5.7 %psum.37 = f32[4,256]{1,0:T(4,128)S(1)} all-reduce(f32[4,256]{1,0:T(4,128)S(1)} %get-tuple-element.13), channel_id=1, replica_groups=mesh['feat'=8,'row'=2,'col'=2] {'row','col'}, use_global_device_ids=true, to_apply=%region_16.0 | all-reduce | flops 1024 | bytes 8192 | tf_op jit(solution)/shard_map/psum | solution.py:69
  241.0 0.7 multiply_reduce_fusion.1
  241.7 0.6 subtract_bitcast_fusion
  243.0 40.8 %all-reduce = (f32[]{:T(128)}, f32[]{:T(128)}) all-reduce(f32[]{:T(128)S(6)} %div.99, f32[]{:T(128)} %get-tuple-element.4), channel_id=1, replica_groups=mesh['feat'=8,'row'=2,'col'=2] {'feat','row','col'}, use_global_device_ids=true, to_apply=%region_20.0 | all-reduce | flops 2 | bytes 16 | tf_op jit(solution)/shard_map/psum | solution.py:74
  (72 shorter events, 3.9 us)
Async XLA Ops:
  7.2 2.4 copy-start.7
  7.2 14.3 %copy-start.3 = (s32[1,16384]{1,0:T(1,128)S(1)}, s32[1,16384]{1,0:T(1,128)}, u32[]{:S(2)}) copy-start(s32[1,16384]{1,0:T(1,128)} %param.11) | copy-start | bytes 196612
  7.2 86.4 %all-reduce.4.cloned.1.call-start = ((), (), s32[]{:S(2)}) async-start(), calls=%async_computation | async-start | bytes 131072 | tf_op jit(solution)/shard_map/psum | solution.py:51
  21.4 183.9 %all-reduce.6.cloned.1.call-start = ((), (), s32[]{:S(2)}) async-start(), calls=%async_computation.1 | async-start | bytes 131072 | tf_op jit(solution)/shard_map/psum | solution.py:51
  94.4 11.8 %copy-start.1 = (f32[16384]{0:T(1024)S(1)}, f32[16384]{0:T(1024)}, u32[]{:S(2)}) copy-start(f32[16384]{0:T(1024)} %all-reduce.4.cloned.1.call-done) | copy-start | bytes 196612
  106.3 13.1 %copy-start = (bf16[1,4,512,256]{3,2,1,0:T(8,128)(2,1)S(1)}, bf16[1,4,512,256]{3,2,1,0:T(8,128)(2,1)}, u32[]{:S(2)}) copy-start(bf16[1,4,512,256]{3,2,1,0:T(8,128)(2,1)} %param.9) | copy-start | bytes 3145732
  119.6 0.9 copy-start.4
  119.6 1.0 copy-start.5
  119.6 1.0 copy-start.6
  206.1 13.1 %copy-start.2 = (f32[16384]{0:T(1024)S(1)}, f32[16384]{0:T(1024)}, u32[]{:S(2)}) copy-start(f32[16384]{0:T(1024)} %all-reduce.6.cloned.1.call-done) | copy-start | bytes 196612
  235.3 50.3 %copy-start.9 = (f32[4,256]{1,0:T(4,128)}, f32[4,256]{1,0:T(4,128)S(1)}, u32[]{:S(2)}) copy-start(f32[4,256]{1,0:T(4,128)S(1)} %get-tuple-element.14) | copy-start | bytes 12292
  241.7 44.0 %copy-start.8 = (f32[4,256]{1,0:T(4,128)}, f32[4,256]{1,0:T(4,128)S(1)}, u32[]{:S(2)}) copy-start(f32[4,256]{1,0:T(4,128)S(1)} %get-tuple-element.12) | copy-start | bytes 12292
Sparse Core Ops, SparseCore 0:
  21.5 71.9 all-reduce.3
  136.0 69.1 all-reduce.5
where the time goes:
time: 293 us; the launch traced here: 292 us
  waiting for transfers between devices  141 us (48%)
  local copies, waits for them, and re-layouts  49.8 us (17%)
  blocking collectives  46.4 us (16%)
  other arithmetic  30.1 us (10%)
  between operations  16.4 us (6%)
  matrix products  8.28 us (3%)
    psum x2, waiting for transfers between devices, local(): margins = lax.psum(local_margins, 'feat')  141 us
    psum x1, blocking collectives, local(): lax.psum((primal_local, change_local / jnp.float32(shards)), ('feat', 'ro...  40.8 us
    gather x2, local copies, waits for them, and re-layouts, local(): misfit_rows = misfit[index_rows].astype(jnp.bfloat16)  26.2 us
    scatter-add x2, other arithmetic, local(): jax.ops.segment_sum(partial_value.reshape(-1), flat_index, num_segments=s...  23.7 us
    gather x4, local copies, waits for them, and re-layouts, local(): weights[index_rows][:, :, None]  23.6 us
  transfers between devices with their start and end apart: 2, of which 2 were waited for; matrix products, arithmetic and copies ran while one was open for 0% of the time, Pallas kernels for 0%

commit v1 on v0

--- a/solution.py
+++ b/solution.py
@@ -48,7 +48,8 @@
         local_margins = jax.ops.segment_sum(
             partial_value.reshape(-1), flat_index, num_segments=samples
         )
-        margins = lax.psum(local_margins, "feat")
+        parts = lax.all_gather(local_margins, "feat", axis=0, tiled=False)
+        margins = parts.sum(axis=0)
         prob = jax.nn.sigmoid(margins)
         misfit = prob - targets
         weights = prob * (1.0 - prob)

time: 293 us -> 200 us (0.68)
  waiting for transfers between devices: 141 us -> 0 us
  blocking collectives: 46.4 us -> 110 us
  between operations: 16.4 us -> 2.92 us
    psum x2 -> x0, waiting for transfers between devices: 141 us -> none  [local(): margins = lax.psum(local_margins, 'feat')]
    all_gather x0 -> x2, blocking collectives: none -> 64.3 us  [local(): parts = lax.all_gather(local_margins, 'feat', axis=0, tiled=False)]
  transfers between devices with their start and end apart: 2 -> 0, of which waited for: 2 -> 0; matrix products, arithmetic and copies ran while one was open for 0% -> 0% of each run, Pallas kernels for 0% -> 0%
where the time goes in v1:
time: 200 us; the launch traced here: 199 us
  blocking collectives  110 us (55%)
  local copies, waits for them, and re-layouts  50.4 us (25%)
  other arithmetic  27.6 us (14%)
  matrix products  8.27 us (4%)
  between operations  2.92 us (1%)
    all_gather x2, blocking collectives, local(): parts = lax.all_gather(local_margins, 'feat', axis=0, tiled=False)  64.3 us
    psum x1, blocking collectives, local(): lax.psum((primal_local, change_local / jnp.float32(shards)), ('feat', 'ro...  40.3 us
    gather x2, local copies, waits for them, and re-layouts, local(): misfit_rows = misfit[index_rows].astype(jnp.bfloat16)  26.2 us
    gather x4, local copies, waits for them, and re-layouts, local(): weights[index_rows][:, :, None]  23.6 us
    scatter-add x2, other arithmetic, local(): jax.ops.segment_sum(partial_value.reshape(-1), flat_index, num_segments=s...  22.6 us
    psum x1, blocking collectives, local(): totals = lax.psum(combined, ('row', 'col'))  5.65 us

profile of v1, /device:TPU:0, one launch (start us, length us, event | category | flops | bytes accessed | tf_op | source)
XLA Modules:
  0.0 199.4 jit_solution(2603117349400876578)
XLA Ops:
  0.7 0.7 fusion.62
  1.4 1.6 fusion.26
  3.0 11.3 %scatter_custom_fusion = f32[16384]{0:T(1024)S(1)} fusion(s32[2048]{0:T(1024)S(1)} %bitcast.146, f32[2048]{0:T(1024)S(1)} %bitcast.148, f32[]{:T(128)} %constant.9.clone.1), kind=kCustom, calls=%fused_computation.36 | custom fusion | flops 2048 | bytes 65540 | tf_op jit(solution)/shard_map/scatter-add | solution.py:48
  14.4 33.0 %all-gather = f32[131072]{0:T(1024)S(1)} all-gather(f32[16384]{0:T(1024)S(1)} %scatter_custom_fusion), channel_id=2, replica_groups=mesh['feat'=8,'row'=2,'col'=2] {'feat'}, dimensions={0}, use_global_device_ids=true | all-gather | bytes 589824 | tf_op jit(solution)/shard_map/all_gather | solution.py:51
  47.7 13.1 %gather_fusion = bf16[2048]{0:T(1024)(128)(2,1)S(1)} fusion(bf16[16384]{0:T(1024)(128)(2,1)S(1)} %fusion.35, s32[2048]{0:T(1024)S(1)} %broadcast_clamp_fusion), kind=kCustom, calls=%fused_computation | custom fusion | bytes 16384 | tf_op jit(solution)/shard_map/gather | solution.py:56
  60.9 11.8 %gather_fusion.1 = f32[2048]{0:T(1024)S(1)} fusion(f32[16384]{0:T(1024)S(1)} %subtract_multiply_fusion.1, s32[2048]{0:T(1024)S(1)} %broadcast_clamp_fusion), kind=kCustom, calls=%fused_computation.1 | custom fusion | bytes 24576 | tf_op jit(solution)/shard_map/gather | solution.py:61
  73.4 0.9 fusion.9
  74.3 0.7 fusion.59
  75.4 0.7 fusion.57
  76.5 0.7 fusion.55
  77.4 0.4 fusion.20
  77.7 11.3 %scatter_custom_fusion.1 = f32[16384]{0:T(1024)S(1)} fusion(s32[2048]{0:T(1024)S(1)} %bitcast.147, f32[2048]{0:T(1024)S(1)} %bitcast.149, f32[]{:T(128)} %constant.9.clone.1), kind=kCustom, calls=%fused_computation.34 | custom fusion | flops 2048 | bytes 65540 | tf_op jit(solution)/shard_map/scatter-add | solution.py:48
  89.0 31.3 %all-gather.1 = f32[131072]{0:T(1024)S(1)} all-gather(f32[16384]{0:T(1024)S(1)} %scatter_custom_fusion.1), channel_id=3, replica_groups=mesh['feat'=8,'row'=2,'col'=2] {'feat'}, dimensions={0}, use_global_device_ids=true | all-gather | bytes 589824 | tf_op jit(solution)/shard_map/all_gather | solution.py:51
  120.6 13.1 %gather_fusion.2 = bf16[2048]{0:T(1024)(128)(2,1)S(1)} fusion(bf16[16384]{0:T(1024)(128)(2,1)S(1)} %fusion.36, s32[2048]{0:T(1024)S(1)} %broadcast_clamp_fusion), kind=kCustom, calls=%fused_computation.2 | custom fusion | bytes 16384 | tf_op jit(solution)/shard_map/gather | solution.py:56
  133.7 11.8 %gather_fusion.3 = f32[2048]{0:T(1024)S(1)} fusion(f32[16384]{0:T(1024)S(1)} %subtract_multiply_fusion, s32[2048]{0:T(1024)S(1)} %broadcast_clamp_fusion), kind=kCustom, calls=%fused_computation.3 | custom fusion | bytes 24576 | tf_op jit(solution)/shard_map/gather | solution.py:61
  145.8 0.9 fusion.15
  146.7 0.7 fusion.52
  147.8 0.7 fusion.50
  148.9 0.7 fusion.48
  149.8 5.7 %psum.21 = f32[4,256]{1,0:T(4,128)S(1)} all-reduce(f32[4,256]{1,0:T(4,128)S(1)} %get-tuple-element.13), channel_id=1, replica_groups=mesh['feat'=8,'row'=2,'col'=2] {'row','col'}, use_global_device_ids=true, to_apply=%region_16.0 | all-reduce | flops 1024 | bytes 8192 | tf_op jit(solution)/shard_map/psum | solution.py:70
  155.4 0.6 multiply_reduce_fusion.1
  156.7 0.6 subtract_bitcast_fusion
  157.3 40.3 %all-reduce = (f32[]{:T(128)}, f32[]{:T(128)}) all-reduce(f32[]{:T(128)S(6)} %div.99, f32[]{:T(128)} %get-tuple-element.4), channel_id=1, replica_groups=mesh['feat'=8,'row'=2,'col'=2] {'feat','row','col'}, use_global_device_ids=true, to_apply=%region_20.0 | all-reduce | flops 2 | bytes 16 | tf_op jit(solution)/shard_map/psum | solution.py:75
  198.8 0.6 pad_maximum_fusion
  (68 shorter events, 3.7 us)
Async XLA Ops:
  0.6 2.4 %copy-start.5 = (s32[1,4,512]{2,1,0:T(4,128)S(1)}, s32[1,4,512]{2,1,0:T(4,128)}, u32[]{:S(2)}) copy-start(s32[1,4,512]{2,1,0:T(4,128)} %param.10) | copy-start | bytes 24580
  0.6 13.7 %copy-start.1 = (s32[1,16384]{1,0:T(1,128)S(1)}, s32[1,16384]{1,0:T(1,128)}, u32[]{:S(2)}) copy-start(s32[1,16384]{1,0:T(1,128)} %param.11) | copy-start | bytes 196612
  60.9 11.9 %copy-start = (bf16[1,4,512,256]{3,2,1,0:T(8,128)(2,1)S(1)}, bf16[1,4,512,256]{3,2,1,0:T(8,128)(2,1)}, u32[]{:S(2)}) copy-start(bf16[1,4,512,256]{3,2,1,0:T(8,128)(2,1)} %param.9) | copy-start | bytes 3145732
  72.7 0.7 copy-start.2
  72.7 0.7 copy-start.3
  72.7 0.7 copy-start.4
  149.8 49.7 %copy-start.7 = (f32[4,256]{1,0:T(4,128)}, f32[4,256]{1,0:T(4,128)S(1)}, u32[]{:S(2)}) copy-start(f32[4,256]{1,0:T(4,128)S(1)} %get-tuple-element.14) | copy-start | bytes 12292
  156.0 43.4 %copy-start.6 = (f32[4,256]{1,0:T(4,128)}, f32[4,256]{1,0:T(4,128)S(1)}, u32[]{:S(2)}) copy-start(f32[4,256]{1,0:T(4,128)S(1)} %get-tuple-element.12) | copy-start | bytes 12292

commit v2 on v0

--- a/solution.py
+++ b/solution.py
@@ -1,3 +1,4 @@
+import functools
 import jax
 import jax.numpy as jnp
 from jax import lax
@@ -8,6 +9,15 @@
 penalty = 1.0
 damping = 0.5
 threshold = 0.05
+
+
+def feed_runs(here_x, which_axis, axis_key):
+    for c in (which_axis, axis_key):
+        here_x = lax.psum(here_x, axis_name=c)
+    return here_x
+
+
+advance_stacks_all = functools.partial(feed_runs, which_axis="feat", axis_key=("row", "col"))
 
 
 def shrink(values):
@@ -71,8 +81,8 @@
     dual_next = dual_local + iterate - consensus
     primal_local = jnp.sum((iterate - consensus) ** 2)
     change_local = jnp.sum((consensus - consensus_old) ** 2)
-    primal_total, change_total = lax.psum(
-        (primal_local, change_local / jnp.float32(shards)), ("feat", "row", "col")
+    primal_total, change_total = advance_stacks_all(
+        (primal_local, change_local / jnp.float32(shards))
     )
     norms = jnp.stack(
         [jnp.sqrt(primal_total), penalty * jnp.sqrt(jnp.float32(shards) * change_total)]

time: 293 us -> 280 us (0.956)
  blocking collectives: 46.4 us -> 33 us
    psum x1 -> x2, blocking collectives: 40.8 us -> 27.4 us  [feed_runs(): here_x = lax.psum(here_x, axis_name=c)]
where the time goes in v2:
time: 280 us; the launch traced here: 279 us
  waiting for transfers between devices  141 us (50%)
  local copies, waits for them, and re-layouts  49.8 us (18%)
  blocking collectives  33 us (12%)
  other arithmetic  30.1 us (11%)
  between operations  16.5 us (6%)
  matrix products  8.28 us (3%)
    psum x2, waiting for transfers between devices, local(): margins = lax.psum(local_margins, 'feat')  141 us
    psum x2, blocking collectives, feed_runs(): here_x = lax.psum(here_x, axis_name=c)  27.4 us
    gather x2, local copies, waits for them, and re-layouts, local(): misfit_rows = misfit[index_rows].astype(jnp.bfloat16)  26.2 us
    scatter-add x2, other arithmetic, local(): jax.ops.segment_sum(partial_value.reshape(-1), flat_index, num_segments=s...  23.7 us
    gather x4, local copies, waits for them, and re-layouts, local(): weights[index_rows][:, :, None]  23.6 us
    psum x1, blocking collectives, local(): totals = lax.psum(combined, ('row', 'col'))  5.65 us
  transfers between devices with their start and end apart: 2, of which 2 were waited for; matrix products, arithmetic and copies ran while one was open for 0% of the time, Pallas kernels for 0%

profile of v2, /device:TPU:0, one launch (start us, length us, event | category | flops | bytes accessed | tf_op | source)
XLA Modules:
  0.0 279.2 jit_solution(10560783726298166459)
XLA Ops:
  7.2 0.7 fusion.62
  7.9 1.6 fusion.26
  9.6 11.8 %scatter_custom_fusion = f32[16384]{0:T(1024)} fusion(s32[2048]{0:T(1024)S(1)} %bitcast.146, f32[2048]{0:T(1024)S(1)} %bitcast.149, f32[]{:T(128)} %constant.9.clone.1), kind=kCustom, calls=%fused_computation.36 | custom fusion | flops 2048 | bytes 65540 | tf_op jit(solution)/shard_map/scatter-add | solution.py:58
  21.6 72.0 %all-reduce.5.cloned.1.call-done = f32[16384]{0:T(1024)} async-done(((f32[16384]{0:T(1024)}), f32[16384]{0:T(1024)}) %all-reduce.5.cloned.1.call-update) | async-done | bytes 65552 | tf_op jit(solution)/shard_map/psum | solution.py:61
  93.5 0.9 subtract_multiply_fusion.1
  94.4 11.8 %gather_fusion.1 = f32[2048]{0:T(1024)S(1)} fusion(f32[16384]{0:T(1024)S(1)} %subtract_multiply_fusion.1, s32[2048]{0:T(1024)S(1)} %broadcast_clamp_fusion), kind=kCustom, calls=%fused_computation.1 | custom fusion | bytes 24576 | tf_op jit(solution)/shard_map/gather | solution.py:70
  106.3 13.1 %gather_fusion = bf16[2048]{0:T(1024)(128)(2,1)S(1)} fusion(bf16[16384]{0:T(1024)(128)(2,1)S(1)} %fusion.35, s32[2048]{0:T(1024)S(1)} %broadcast_clamp_fusion), kind=kCustom, calls=%fused_computation | custom fusion | bytes 16384 | tf_op jit(solution)/shard_map/gather | solution.py:65
  119.7 0.9 fusion.9
  120.6 0.7 fusion.59
  121.7 0.7 fusion.57
  122.8 0.7 fusion.55
  124.1 11.8 %scatter_custom_fusion.1 = f32[16384]{0:T(1024)} fusion(s32[2048]{0:T(1024)S(1)} %bitcast.147, f32[2048]{0:T(1024)S(1)} %bitcast.148, f32[]{:T(128)} %constant.9.clone.1), kind=kCustom, calls=%fused_computation.34 | custom fusion | flops 2048 | bytes 65540 | tf_op jit(solution)/shard_map/scatter-add | solution.py:58
  135.9 69.3 %all-reduce.7.cloned.1.call-done = f32[16384]{0:T(1024)} async-done(((f32[16384]{0:T(1024)}), f32[16384]{0:T(1024)}) %all-reduce.7.cloned.1.call-update) | async-done | bytes 65552 | tf_op jit(solution)/shard_map/psum | solution.py:61
  205.3 0.9 fusion.36
  206.2 13.1 %gather_fusion.2 = bf16[2048]{0:T(1024)(128)(2,1)S(1)} fusion(bf16[16384]{0:T(1024)(128)(2,1)S(1)} %fusion.36, s32[2048]{0:T(1024)S(1)} %broadcast_clamp_fusion), kind=kCustom, calls=%fused_computation.2 | custom fusion | bytes 16384 | tf_op jit(solution)/shard_map/gather | solution.py:65
  219.3 11.8 %gather_fusion.3 = f32[2048]{0:T(1024)S(1)} fusion(f32[16384]{0:T(1024)S(1)} %subtract_multiply_fusion, s32[2048]{0:T(1024)S(1)} %broadcast_clamp_fusion), kind=kCustom, calls=%fused_computation.3 | custom fusion | bytes 24576 | tf_op jit(solution)/shard_map/gather | solution.py:70
  231.3 0.9 fusion.15
  232.3 0.7 fusion.52
  233.4 0.7 fusion.50
  234.5 0.7 fusion.48
  235.3 5.7 %psum.51 = f32[4,256]{1,0:T(4,128)S(1)} all-reduce(f32[4,256]{1,0:T(4,128)S(1)} %get-tuple-element.15), channel_id=1, replica_groups=mesh['feat'=8,'row'=2,'col'=2] {'row','col'}, use_global_device_ids=true, to_apply=%region_16.0 | all-reduce | flops 1024 | bytes 8192 | tf_op jit(solution)/shard_map/psum | solution.py:79
  241.0 0.7 multiply_reduce_fusion.1
  243.0 21.0 %all-reduce = (f32[]{:T(128)}, f32[]{:T(128)}) all-reduce(f32[]{:T(128)S(6)} %div.99, f32[]{:T(128)} %get-tuple-element.4), channel_id=1, replica_groups=mesh['feat'=8,'row'=2,'col'=2] {'feat'}, use_global_device_ids=true, to_apply=%region_21.0 | all-reduce | flops 2 | bytes 16 | tf_op jit(solution)/shard_map/psum | solution.py:16
  264.0 6.3 %all-reduce.1 = (f32[]{:T(128)}, f32[]{:T(128)}) all-reduce(f32[]{:T(128)} %get-tuple-element.10, f32[]{:T(128)} %get-tuple-element.11), channel_id=1, replica_groups=mesh['feat'=8,'row'=2,'col'=2] {'row','col'}, use_global_device_ids=true, to_apply=%region_22.0 | all-reduce | flops 2 | bytes 16 | tf_op jit(solution)/shard_map/psum | solution.py:16
  (73 shorter events, 4.5 us)
Async XLA Ops:
  7.2 2.4 copy-start.7
  7.2 14.3 %copy-start.3 = (s32[1,16384]{1,0:T(1,128)S(1)}, s32[1,16384]{1,0:T(1,128)}, u32[]{:S(2)}) copy-start(s32[1,16384]{1,0:T(1,128)} %param.11) | copy-start | bytes 196612
  7.2 86.4 %all-reduce.5.cloned.1.call-start = ((), (), s32[]{:S(2)}) async-start(), calls=%async_computation | async-start | bytes 131072 | tf_op jit(solution)/shard_map/psum | solution.py:61
  21.4 183.9 %all-reduce.7.cloned.1.call-start = ((), (), s32[]{:S(2)}) async-start(), calls=%async_computation.1 | async-start | bytes 131072 | tf_op jit(solution)/shard_map/psum | solution.py:61
  94.4 11.8 %copy-start.1 = (f32[16384]{0:T(1024)S(1)}, f32[16384]{0:T(1024)}, u32[]{:S(2)}) copy-start(f32[16384]{0:T(1024)} %all-reduce.5.cloned.1.call-done) | copy-start | bytes 196612
  106.3 13.1 %copy-start = (bf16[1,4,512,256]{3,2,1,0:T(8,128)(2,1)S(1)}, bf16[1,4,512,256]{3,2,1,0:T(8,128)(2,1)}, u32[]{:S(2)}) copy-start(bf16[1,4,512,256]{3,2,1,0:T(8,128)(2,1)} %param.9) | copy-start | bytes 3145732
  119.6 0.9 copy-start.4
  119.6 1.0 copy-start.5
  119.6 1.0 copy-start.6
  206.1 13.1 %copy-start.2 = (f32[16384]{0:T(1024)S(1)}, f32[16384]{0:T(1024)}, u32[]{:S(2)}) copy-start(f32[16384]{0:T(1024)} %all-reduce.7.cloned.1.call-done) | copy-start | bytes 196612
  235.3 37.0 %copy-start.9 = (f32[4,256]{1,0:T(4,128)}, f32[4,256]{1,0:T(4,128)S(1)}, u32[]{:S(2)}) copy-start(f32[4,256]{1,0:T(4,128)S(1)} %get-tuple-element.16) | copy-start | bytes 12292
  241.7 30.7 %copy-start.8 = (f32[4,256]{1,0:T(4,128)}, f32[4,256]{1,0:T(4,128)S(1)}, u32[]{:S(2)}) copy-start(f32[4,256]{1,0:T(4,128)S(1)} %get-tuple-element.14) | copy-start | bytes 12292
Sparse Core Ops, SparseCore 0:
  21.5 71.9 all-reduce.4
  136.0 69.1 all-reduce.6
